TPU v7x, 32 devices: a whole 2x2x4 slice. The times are simulated.
32 devices in a mesh: grp: 4 (over z), dev: 8 (over y, x, core).
Axes of the slice: x: 2, y: 2, z: 4, core: 2. Of those that a mesh axis runs over, the one named last changes fastest.
Arguments:
- amounts: float32 [64, 524288], P('dev', 'grp'), may hold values from -0.06 to 0.06, as said below
Outputs:
- offsets: float32 [64, 524288], P(None, ('grp', 'dev'))
Inputs may be any that keep to these rules, and one draw needn't show every extreme that they name: `amounts`: each entry lies within 0.06 of zero.
All inputs are finite; a program needn't handle non-finite values.
Results may differ from a plain program's by a relative error of at most 0.00095.
Values sent between devices are 32-bit elements; how exact they have to be, the bound alone decides.
No kernel may reach another device: no remote copies, remote signals or barrier semaphores. Data moves between devices by JAX's collectives and lax.ppermute only.
A program may use at most 64 MiB of HBM per device.

v0:
```python
import functools

import jax
import jax.numpy as jnp
from jax import lax
from jax.experimental import pallas as pl
from jax.experimental.pallas import tpu as pltpu
from jax.sharding import PartitionSpec as P


LANES = 128
VMEM = pl.BlockSpec(memory_space=pltpu.VMEM)
HBM = pl.BlockSpec(memory_space=pltpu.HBM)


def params(mib, flops):
    return {
        "compiler_params": pltpu.CompilerParams(vmem_limit_bytes=mib << 20),
        "cost_estimate": pl.CostEstimate(flops=flops, bytes_accessed=0, transcendentals=0),
    }


def shape(*dims):
    return jax.ShapeDtypeStruct(dims, jnp.float32)


X_OR_Y, Y_OR_X = (2, 4), (4, 2)
X_OTHER, Y_OTHER, DIAGONAL, DIAGONAL_OTHER, CORE, SELF = ((k, k) for k in (3, 5, 6, 7, 1, 0))


def partner(k):
    me = lax.axis_index("dev")
    return me ^ (k[0] + (me & 1) * (k[1] - k[0]))


def swap(value, k):
    count = lax.axis_size("dev")
    return lax.ppermute(value, "dev", [(i, i ^ k[i & 1]) for i in range(count)])


def shift_later(value, by):
    count = lax.axis_size("grp")
    return lax.ppermute(value, "grp", [(i, i + by) for i in range(count - by)])


def fetch(a_ref, ks, refs, sems):
    rows = a_ref.shape[1] // lax.axis_size("dev")
    copies = []
    for n, k in enumerate(ks):
        start = pl.multiple_of(partner(k) * rows, rows)
        copy = pltpu.make_async_copy(a_ref.at[:, pl.ds(start, rows)], refs[n], sems.at[n])
        copy.start()
        copies.append(copy)
    return copies


def grab_kernel(ks, a_ref, *refs):
    for copy in fetch(a_ref, ks, refs[:-1], refs[-1]):
        copy.wait()


def grab(a, ks):
    chans, length = a.shape
    return pl.pallas_call(
        functools.partial(grab_kernel, ks),
        out_shape=[shape(chans, length // lax.axis_size("dev"))] * len(ks),
        in_specs=[HBM],
        out_specs=[VMEM] * len(ks),
        scratch_shapes=[pltpu.SemaphoreType.DMA((len(ks),))],
        name="grab",
        **params(8, 1000000),
    )(a)


def piece_sum(ref):
    chans, rows = ref.shape
    width = 8 * LANES

    def step(n, acc):
        at = pl.multiple_of(n * width, width)
        return acc + ref[:, pl.ds(at, width)]

    acc = lax.fori_loop(1, rows // width, step, ref[:, :width], unroll=True)
    total = acc[:, :LANES]
    for n in range(1, 8):
        total = total + acc[:, n * LANES : (n + 1) * LANES]
    return jnp.broadcast_to(jnp.sum(total, axis=1, keepdims=True), (chans, LANES))


def sums_kernel(ahead, rest, a_ref, *refs):
    ahead_refs, refs = refs[: len(ahead)], refs[len(ahead) :]
    rest_refs, (total_ref, sums_ref, sems) = refs[: len(rest)], refs[len(rest) :]
    chans = a_ref.shape[0]
    copies = fetch(a_ref, rest, rest_refs, sems)
    total = jnp.zeros((chans, LANES), jnp.float32)
    for k, ref, copy in zip(ahead + rest, ahead_refs + rest_refs, [None] * len(ahead) + copies):
        if copy is not None:
            copy.wait()
        this = piece_sum(ref)
        total = total + this
        sums_ref[pl.ds(pl.multiple_of(partner(k) * chans, chans), chans), :] = this
    total_ref[...] = total


def sums(a, ahead, pieces, rest):
    chans, rows = pieces[0].shape
    return pl.pallas_call(
        functools.partial(sums_kernel, ahead, rest),
        out_shape=[shape(chans, rows)] * len(rest)
        + [shape(chans, LANES), shape(chans * lax.axis_size("dev"), LANES)],
        in_specs=[HBM] + [VMEM] * len(ahead),
        out_specs=[VMEM] * (len(rest) + 2),
        scratch_shapes=[pltpu.SemaphoreType.DMA((len(rest),))],
        name="sums",
        **params(8, 40000000),
    )(a, *pieces)


def carry_kernel(apart, inside, shifts, sums_ref, *refs):
    group_refs, refs = refs[:shifts], refs[shifts:]
    old_refs, refs = refs[: len(inside)], refs[len(inside) :]
    new_refs, apart_refs, carry_ref = refs[: len(inside)], refs[len(inside) : -1], refs[-1]
    chans = group_refs[0].shape[0]
    count = sums_ref.shape[0] // chans
    carry = jnp.zeros((chans, LANES), jnp.float32)
    for ref in group_refs:
        carry = carry + ref[...]
    for e in range(count):
        carry_ref[e * chans : (e + 1) * chans, :] = carry
        carry = carry + sums_ref[e * chans : (e + 1) * chans, :]

    def carry_of(k):
        return carry_ref[pl.ds(pl.multiple_of(partner(k) * chans, chans), chans), :]

    lane = lax.broadcasted_iota(jnp.int32, (chans, LANES), 1)
    for n, k in enumerate(inside):
        at = old_refs[n].shape[1] - LANES
        new_refs[n][:, at:] = jnp.where(lane == LANES - 1, carry_of(k), old_refs[n][:, at:])
    for n, k in enumerate(apart):
        apart_refs[n][...] = carry_of(k)


def carries(chunk_sums, groups, inside, pieces, apart):
    chans = pieces[0].shape[0]
    return pl.pallas_call(
        functools.partial(carry_kernel, apart, inside, len(groups)),
        out_shape=[shape(*piece.shape) for piece in pieces] + [shape(chans, LANES)] * len(apart),
        in_specs=[VMEM] * (1 + len(groups) + len(inside)),
        out_specs=[VMEM] * (len(inside) + len(apart)),
        scratch_shapes=[pltpu.VMEM(chunk_sums.shape, jnp.float32)],
        input_output_aliases={1 + len(groups) + n: n for n in range(len(inside))},
        name="carries",
        **params(8, 10000000),
    )(chunk_sums, *groups, *pieces)


STEP = 32


def scan_piece(piece_ref, carry, held_ref, done):
    chans, rows = piece_ref.shape
    many = STEP
    width = many * LANES
    row = lax.broadcasted_iota(jnp.int32, (LANES, 2 * LANES), 0)
    col = lax.broadcasted_iota(jnp.int32, (LANES, 2 * LANES), 1)
    mask = jnp.where(row < col, 1.0, 0.0).astype(jnp.bfloat16)
    mask2 = jnp.concatenate([mask, mask], axis=0)
    for at in range(0, rows, width):
        x = piece_ref[:, at : at + width]
        x = jnp.concatenate([x[:, j * LANES : (j + 1) * LANES] for j in range(many)], axis=0)
        high = x.astype(jnp.bfloat16)
        rest = x - high.astype(jnp.float32)
        mid = rest.astype(jnp.bfloat16)
        low = (rest - mid.astype(jnp.float32)).astype(jnp.bfloat16)
        both = jnp.concatenate([high, mid], axis=1)
        res = jnp.dot(both, mask2, preferred_element_type=jnp.float32)
        res = res + jnp.dot(low, mask, preferred_element_type=jnp.float32)
        for j in range(many):
            part = res[j * chans : (j + 1) * chans]
            start = at + j * LANES
            held_ref[:, start : start + LANES] = part[:, :LANES] + carry
            carry = carry + part[:, LANES:]
        done(at, width)


def scan_kernel(k, aliased, apart, *refs):
    piece_ref, *refs = refs[aliased:]
    chans, rows = piece_ref.shape
    if apart:
        carry_ref, *refs = refs
        carry = carry_ref[...]
    else:
        last = piece_ref[:, rows - LANES :]
        carry = jnp.broadcast_to(last[:, LANES - 1 :], last.shape)
    out_ref, held_ref, sems = refs
    start = pl.multiple_of(partner(k) * chans, chans)
    copies = []

    def copy_out(at, width):
        target = out_ref.at[pl.ds(start, chans), pl.ds(at, width)]
        copies.append(pltpu.make_async_copy(held_ref.at[:, pl.ds(at, width)], target, sems.at[at // width]))
        copies[-1].start()

    scan_piece(piece_ref, carry, held_ref, copy_out)
    for copy in copies:
        copy.wait()


def scan(out, k, piece, carry=None):
    chans, rows = piece.shape
    inputs = [piece] if carry is None else [piece, carry]
    before = [] if out is None else [out]
    return pl.pallas_call(
        functools.partial(scan_kernel, k, len(before), carry is not None),
        out_shape=shape(chans * lax.axis_size("dev"), rows),
        in_specs=[HBM] * len(before) + [VMEM] * len(inputs),
        out_specs=HBM,
        scratch_shapes=[
            pltpu.VMEM((chans, rows), jnp.float32),
            pltpu.SemaphoreType.DMA((rows // (STEP * LANES),)),
        ],
        input_output_aliases={0: 0} if before else {},
        name="scan",
        **params(8, 20000000),
    )(*before, *inputs)


def scan_ahead_kernel(piece_ref, carry_ref, out_ref):
    scan_piece(piece_ref, carry_ref[...], out_ref, lambda at, width: None)


def scan_ahead(piece, carry):
    return pl.pallas_call(
        scan_ahead_kernel,
        out_shape=shape(*piece.shape),
        in_specs=[VMEM] * 2,
        out_specs=VMEM,
        name="scan_ahead",
        **params(8, 20000000),
    )(piece, carry)


def place_kernel(k, _, piece_ref, out_ref, sem):
    chans = piece_ref.shape[0]
    start = pl.multiple_of(partner(k) * chans, chans)
    copy = pltpu.make_async_copy(piece_ref, out_ref.at[pl.ds(start, chans), :], sem)
    copy.start()
    copy.wait()


def place(out, k, piece):
    return pl.pallas_call(
        functools.partial(place_kernel, k),
        out_shape=shape(*out.shape),
        in_specs=[HBM, VMEM],
        out_specs=HBM,
        scratch_shapes=[pltpu.SemaphoreType.DMA],
        input_output_aliases={0: 0},
        name="place",
        **params(8, 1000000),
    )(out, piece)


AHEAD, EARLY = [X_OR_Y, Y_OR_X], [Y_OTHER, X_OTHER]
LATE, LAST = [DIAGONAL, CORE], DIAGONAL_OTHER


def overlapped(a):
    a = pltpu.with_memory_space_constraint(a, pltpu.HBM)
    piece = dict(zip(AHEAD, grab(a, AHEAD)))
    rest = EARLY + LATE + [LAST, SELF]
    *pieces, total, chunk_sums = sums(a, AHEAD, [piece[k] for k in AHEAD], rest)
    piece.update(zip(rest, pieces))
    got = {k: swap(piece[k], k) for k in AHEAD + EARLY}
    groups = [shift_later(total, by) for by in range(1, lax.axis_size("grp"))]
    apart = AHEAD + EARLY + [LAST, SELF]
    made = carries(chunk_sums, groups, LATE, [piece[k] for k in LATE], apart)
    carry = dict(zip(apart, made[len(LATE) :]))
    got_carry = {k: swap(carry[k], k) for k in AHEAD + EARLY}
    for k, value in zip(LATE, made):
        got[k] = swap(value, k)
    got[LAST] = swap(scan_ahead(piece[LAST], carry[LAST]), LAST)
    out = scan(None, SELF, piece[SELF], carry[SELF])
    for k in AHEAD + EARLY:
        out = scan(out, k, got[k], got_carry[k])
    for k in reversed(LATE):
        out = scan(out, k, got[k])
    return place(out, LAST, got[LAST])


def plain(a):
    count = lax.axis_size("dev")
    chans, length = a.shape
    rows = length // count
    sums = jnp.sum(a.reshape(chans, count, rows), axis=2)
    carry = jnp.cumsum(sums, axis=1) - sums
    total = jnp.sum(sums, axis=1)
    for by in range(1, lax.axis_size("grp")):
        carry = carry + shift_later(total, by)[:, None]
    carry = lax.all_to_all(carry, "dev", split_axis=1, concat_axis=0, tiled=True)
    x = lax.all_to_all(a, "dev", split_axis=1, concat_axis=0, tiled=True)
    blocks = x.reshape(chans * count, rows // LANES, LANES)
    row = lax.broadcasted_iota(jnp.int32, (LANES, LANES), 0)
    col = lax.broadcasted_iota(jnp.int32, (LANES, LANES), 1)
    within = jnp.dot(
        blocks, (row < col).astype(jnp.float32), precision=lax.Precision.HIGHEST,
        preferred_element_type=jnp.float32,
    )
    block_sums = jnp.sum(blocks, axis=2)
    starts = jnp.cumsum(block_sums, axis=1) - block_sums + carry
    return (within + starts[:, :, None]).reshape(chans * count, rows)


def local(a):
    chans, length = a.shape
    fits = lax.axis_size("dev") == 8 and lax.axis_size("grp") > 1
    if fits and chans == 8 and length % (8 * STEP * LANES) == 0:
        return overlapped(a)
    return plain(a)


def solution(mesh):
    return jax.shard_map(
        local,
        mesh=mesh,
        in_specs=(P("dev", "grp"),),
        out_specs=P(None, ("grp", "dev")),
        check_vma=False,
    )
```

profile of v0, /device:TPU:0, one launch (start us, length us, event | category | flops | bytes accessed | tf_op | source)
XLA Modules:
  0.0 72.5 jit_solution(415787906085768158)
XLA Ops:
  0.0 1.2 %grab.1 = (f32[8,16384]{1,0:T(8,128)S(1)}, f32[8,16384]{1,0:T(8,128)S(1)}) custom-call(f32[8,131072]{1,0:T(8,128)} %a_ref.3), custom_call_target="tpu_custom_call" | custom-call | flops 1000000 | tf_op jit(solution)/shard_map/grab/pallas_call | solution.py:64
  1.2 3.0 %collective-permute-start.3 = (f32[8,16384]{1,0:T(8,128)S(1)}, f32[8,16384]{1,0:T(8,128)S(1)}, u32[]{:S(2)}, u32[]{:S(2)}) collective-permute-start(f32[8,16384]{1,0:T(8,128)S(1)} %get-tuple-element.23.refs_0_), channel_id=1, source_target_pairs={{0,2},{1,5},{2,0},{3,7},{4,6},{5,1},{6,4},{7,3},{8,10},{9,13},{10,... | collective-permute-start | bytes 1572872 | tf_op jit(solution)/shard_map/ppermute | solution.py:38
  4.3 1.5 %collective-permute-start.5 = (f32[8,16384]{1,0:T(8,128)S(1)}, f32[8,16384]{1,0:T(8,128)S(1)}, u32[]{:S(2)}, u32[]{:S(2)}) collective-permute-start(f32[8,16384]{1,0:T(8,128)S(1)} %get-tuple-element.24.refs_1_), channel_id=1, source_target_pairs={{0,4},{1,3},{2,6},{3,1},{4,0},{5,7},{6,2},{7,5},{8,12},{9,11},{10,... | collective-permute-start | bytes 1572872 | tf_op jit(solution)/shard_map/ppermute | solution.py:38
  5.8 2.0 %sums.1 = (f32[8,16384]{1,0:T(8,128)S(1)}, f32[8,16384]{1,0:T(8,128)S(1)}, f32[8,16384]{1,0:T(8,128)S(1)}, f32[8,16384]{1,0:T(8,128)S(1)}, f32[8,16384]{1,0:T(8,...) custom-call(f32[8,131072]{1,0:T(8,128)} %a_ref.3, ...), custom_call_target="tpu_custom_call" | custom-call | flops 40000000 | tf_op jit(solution)/shard_map/sums/pallas_call | solution.py:107
  7.8 5.5 %collective-permute-start.2 = (f32[8,128]{1,0:T(8,128)S(1)}, f32[8,128]{1,0:T(8,128)S(1)}, u32[]{:S(2)}, u32[]{:S(2)}) collective-permute-start(f32[8,128]{1,0:T(8,128)S(1)} %get-tuple-element.27), channel_id=1, source_target_pairs={{0,24},{1,25},{2,26},{3,27},{4,28},{5,29},{6,30},{7,31}} | collective-permute-start | bytes 12296 | tf_op jit(solution)/shard_map/ppermute | solution.py:43
  13.3 1.3 %collective-permute-start.1 = (f32[8,128]{1,0:T(8,128)S(1)}, f32[8,128]{1,0:T(8,128)S(1)}, u32[]{:S(2)}, u32[]{:S(2)}) collective-permute-start(f32[8,128]{1,0:T(8,128)S(1)} %get-tuple-element.27), channel_id=1, source_target_pairs={{0,16},{8,24},{1,17},{9,25},{2,18},{10,26},{3,19},{11,27},{4,20},{... | collective-permute-start | bytes 12296 | tf_op jit(solution)/shard_map/ppermute | solution.py:43
  14.6 2.5 %collective-permute-start = (f32[8,128]{1,0:T(8,128)S(1)}, f32[8,128]{1,0:T(8,128)S(1)}, u32[]{:S(2)}, u32[]{:S(2)}) collective-permute-start(f32[8,128]{1,0:T(8,128)S(1)} %get-tuple-element.27), channel_id=1, source_target_pairs={{0,8},{8,16},{16,24},{1,9},{9,17},{17,25},{2,10},{10,18},{18,26},{... | collective-permute-start | bytes 12296 | tf_op jit(solution)/shard_map/ppermute | solution.py:43
  17.1 0.0 collective-permute-done.2.refs_2_
  17.1 0.0 collective-permute-done.1.refs_1_
  17.1 1.3 %collective-permute-done.refs_0_ = f32[8,128]{1,0:T(8,128)S(1)} collective-permute-done((f32[8,128]{1,0:T(8,128)S(1)}, f32[8,128]{1,0:T(8,128)S(1)}, u32[]{:S(2)}, u32[]{:S(2)}) %collective-permute-start) | collective-permute-done | bytes 4128 | tf_op jit(solution)/shard_map/ppermute | solution.py:43
  18.4 0.6 collective-permute-start.4
  19.0 0.0 collective-permute-start.7
  19.0 0.5 collective-permute-start.6
  19.5 2.6 %collective-permute-done.4.refs_2_ = f32[8,128]{1,0:T(8,128)S(1)} collective-permute-done((f32[8,128]{1,0:T(8,128)S(1)}, f32[8,128]{1,0:T(8,128)S(1)}, u32[]{:S(2)}, u32[]{:S(2)}) %collective-permute-start.4) | collective-permute-done | bytes 4128 | tf_op jit(solution)/shard_map/ppermute | solution.py:38
  22.1 0.0 collective-permute-start.8
  22.1 9.4 %collective-permute-done.6.refs_2_ = f32[8,128]{1,0:T(8,128)S(1)} collective-permute-done((f32[8,128]{1,0:T(8,128)S(1)}, f32[8,128]{1,0:T(8,128)S(1)}, u32[]{:S(2)}, u32[]{:S(2)}) %collective-permute-start.6) | collective-permute-done | bytes 4128 | tf_op jit(solution)/shard_map/ppermute | solution.py:38
  31.4 0.0 collective-permute-start.9
  31.4 1.0 %collective-permute-done.8.refs_2_ = f32[8,128]{1,0:T(8,128)S(1)} collective-permute-done((f32[8,128]{1,0:T(8,128)S(1)}, f32[8,128]{1,0:T(8,128)S(1)}, u32[]{:S(2)}, u32[]{:S(2)}) %collective-permute-start.8) | collective-permute-done | bytes 4128 | tf_op jit(solution)/shard_map/ppermute | solution.py:38
  32.4 0.6 collective-permute-start.11
  33.0 0.0 collective-permute-done.3.refs_1_
  33.0 2.4 %collective-permute-start.12 = (f32[8,16384]{1,0:T(8,128)S(1)}, f32[8,16384]{1,0:T(8,128)S(1)}, u32[]{:S(2)}, u32[]{:S(2)}) collective-permute-start(f32[8,16384]{1,0:T(8,128)S(1)} %get-tuple-element.38), channel_id=1, source_target_pairs={{0,6},{1,7},{2,4},{3,5},{4,2},{5,3},{6,0},{7,1},{8,14},{9,15},{10,... | collective-permute-start | bytes 1572872 | tf_op jit(solution)/shard_map/ppermute | solution.py:38
  35.4 0.5 scan_ahead.1
  35.9 0.0 collective-permute-done.5.refs_1_
  35.9 0.1 collective-permute-start.13
  36.0 1.2 %scan.7.refs_0_ = f32[64,16384]{1,0:T(8,128)} custom-call(f32[8,16384]{1,0:T(8,128)S(1)} %get-tuple-element.25.refs_0_, f32[8,128]{1,0:T(8,128)S(1)} %get-tuple-element.30.refs_1_), custom_call_target="tpu_custom_call" | custom-call | flops 20000000 | tf_op jit(solution)/shard_map/scan/pallas_call | solution.py:213
  37.1 0.0 collective-permute-done.7.refs_1_
  37.1 1.3 %collective-permute-start.10 = (f32[8,128]{1,0:T(8,128)S(1)}, f32[8,128]{1,0:T(8,128)S(1)}, u32[]{:S(2)}, u32[]{:S(2)}) collective-permute-start(f32[8,128]{1,0:T(8,128)S(1)} %get-tuple-element.36), channel_id=1, source_target_pairs={{0,3},{1,2},{2,1},{3,0},{4,7},{5,6},{6,5},{7,4},{8,11},{9,10},{10,... | collective-permute-start | bytes 12296 | tf_op jit(solution)/shard_map/ppermute | solution.py:38
  38.4 1.2 %scan.8.refs_0_ = f32[64,16384]{1,0:T(8,128)} custom-call(f32[64,16384]{1,0:T(8,128)} %scan.7.refs_0_, f32[8,16384]{1,0:T(8,128)S(1)} %collective-permute-done.3.refs_1_, f32[8,128]{1,0:T(8,128)S(1)} %collective-permute-done.4.refs_2_), custom_call_target="tpu_custom_call", output_to_operand_aliasing={{}: (0, {})} | custom-call | flops 20000000 | tf_op jit(solution)/shard_map/scan/pallas_call | solution.py:213
  39.6 1.2 %scan.9.refs_0_ = f32[64,16384]{1,0:T(8,128)} custom-call(f32[64,16384]{1,0:T(8,128)} %scan.8.refs_0_, f32[8,16384]{1,0:T(8,128)S(1)} %collective-permute-done.5.refs_1_, f32[8,128]{1,0:T(8,128)S(1)} %collective-permute-done.6.refs_2_), custom_call_target="tpu_custom_call", output_to_operand_aliasing={{}: (0, {})} | custom-call | flops 20000000 | tf_op jit(solution)/shard_map/scan/pallas_call | solution.py:213
  40.8 1.2 %scan.10.refs_0_ = f32[64,16384]{1,0:T(8,128)} custom-call(f32[64,16384]{1,0:T(8,128)} %scan.9.refs_0_, f32[8,16384]{1,0:T(8,128)S(1)} %collective-permute-done.7.refs_1_, f32[8,128]{1,0:T(8,128)S(1)} %collective-permute-done.8.refs_2_), custom_call_target="tpu_custom_call", output_to_operand_aliasing={{}: (0, {})} | custom-call | flops 20000000 | tf_op jit(solution)/shard_map/scan/pallas_call | solution.py:213
  41.9 26.2 %collective-permute-done.10.refs_2_ = f32[8,128]{1,0:T(8,128)S(1)} collective-permute-done((f32[8,128]{1,0:T(8,128)S(1)}, f32[8,128]{1,0:T(8,128)S(1)}, u32[]{:S(2)}, u32[]{:S(2)}) %collective-permute-start.10) | collective-permute-done | bytes 4128 | tf_op jit(solution)/shard_map/ppermute | solution.py:38
  68.2 0.0 collective-permute-done.9.refs_1_
  68.2 1.2 %scan.11.refs_0_ = f32[64,16384]{1,0:T(8,128)} custom-call(f32[64,16384]{1,0:T(8,128)} %scan.10.refs_0_, f32[8,16384]{1,0:T(8,128)S(1)} %collective-permute-done.9.refs_1_, f32[8,128]{1,0:T(8,128)S(1)} %collective-permute-done.10.refs_2_), custom_call_target="tpu_custom_call", output_to_operand_aliasing={{}: (0, {})} | custom-call | flops 20000000 | tf_op jit(solution)/shard_map/scan/pallas_call | solution.py:213
  69.3 0.0 collective-permute-done.11.refs_1_
  69.4 1.2 %scan.12.refs_0_ = f32[64,16384]{1,0:T(8,128)} custom-call(f32[64,16384]{1,0:T(8,128)} %scan.11.refs_0_, f32[8,16384]{1,0:T(8,128)S(1)} %collective-permute-done.11.refs_1_), custom_call_target="tpu_custom_call", output_to_operand_aliasing={{}: (0, {})} | custom-call | flops 20000000 | tf_op jit(solution)/shard_map/scan/pallas_call | solution.py:213
  70.5 0.0 collective-permute-done.12.refs_1_
  70.5 1.2 %scan.13._ = f32[64,16384]{1,0:T(8,128)} custom-call(f32[64,16384]{1,0:T(8,128)} %scan.12.refs_0_, f32[8,16384]{1,0:T(8,128)S(1)} %collective-permute-done.12.refs_1_), custom_call_target="tpu_custom_call", output_to_operand_aliasing={{}: (0, {})} | custom-call | flops 20000000 | tf_op jit(solution)/shard_map/scan/pallas_call | solution.py:213
  71.7 0.0 collective-permute-done.13.piece_ref
  71.7 0.8 %place.1 = f32[64,16384]{1,0:T(8,128)} custom-call(f32[64,16384]{1,0:T(8,128)} %scan.13._, f32[8,16384]{1,0:T(8,128)S(1)} %collective-permute-done.13.piece_ref), custom_call_target="tpu_custom_call", output_to_operand_aliasing={{}: (0, {})} | custom-call | flops 1000000 | tf_op jit(solution)/shard_map/place/pallas_call | solution.py:252
  (1 shorter events, 0.0 us)
Async XLA Ops:
  1.2 31.8 %collective-permute-start.3 = (f32[8,16384]{1,0:T(8,128)S(1)}, f32[8,16384]{1,0:T(8,128)S(1)}, u32[]{:S(2)}, u32[]{:S(2)}) collective-permute-start(f32[8,16384]{1,0:T(8,128)S(1)} %get-tuple-element.23.refs_0_), channel_id=1, source_target_pairs={{0,2},{1,5},{2,0},{3,7},{4,6},{5,1},{6,4},{7,3},{8,10},{9,13},{10,... | collective-permute-start | bytes 1572872 | tf_op jit(solution)/shard_map/ppermute | solution.py:38
  4.3 31.6 %collective-permute-start.5 = (f32[8,16384]{1,0:T(8,128)S(1)}, f32[8,16384]{1,0:T(8,128)S(1)}, u32[]{:S(2)}, u32[]{:S(2)}) collective-permute-start(f32[8,16384]{1,0:T(8,128)S(1)} %get-tuple-element.24.refs_1_), channel_id=1, source_target_pairs={{0,4},{1,3},{2,6},{3,1},{4,0},{5,7},{6,2},{7,5},{8,12},{9,11},{10,... | collective-permute-start | bytes 1572872 | tf_op jit(solution)/shard_map/ppermute | solution.py:38
  7.8 9.3 %collective-permute-start.2 = (f32[8,128]{1,0:T(8,128)S(1)}, f32[8,128]{1,0:T(8,128)S(1)}, u32[]{:S(2)}, u32[]{:S(2)}) collective-permute-start(f32[8,128]{1,0:T(8,128)S(1)} %get-tuple-element.27), channel_id=1, source_target_pairs={{0,24},{1,25},{2,26},{3,27},{4,28},{5,29},{6,30},{7,31}} | collective-permute-start | bytes 12296 | tf_op jit(solution)/shard_map/ppermute | solution.py:43
  13.3 3.8 %collective-permute-start.1 = (f32[8,128]{1,0:T(8,128)S(1)}, f32[8,128]{1,0:T(8,128)S(1)}, u32[]{:S(2)}, u32[]{:S(2)}) collective-permute-start(f32[8,128]{1,0:T(8,128)S(1)} %get-tuple-element.27), channel_id=1, source_target_pairs={{0,16},{8,24},{1,17},{9,25},{2,18},{10,26},{3,19},{11,27},{4,20},{... | collective-permute-start | bytes 12296 | tf_op jit(solution)/shard_map/ppermute | solution.py:43
  14.6 3.8 %collective-permute-start = (f32[8,128]{1,0:T(8,128)S(1)}, f32[8,128]{1,0:T(8,128)S(1)}, u32[]{:S(2)}, u32[]{:S(2)}) collective-permute-start(f32[8,128]{1,0:T(8,128)S(1)} %get-tuple-element.27), channel_id=1, source_target_pairs={{0,8},{8,16},{16,24},{1,9},{9,17},{17,25},{2,10},{10,18},{18,26},{... | collective-permute-start | bytes 12296 | tf_op jit(solution)/shard_map/ppermute | solution.py:43
  18.4 3.7 %collective-permute-start.4 = (f32[8,128]{1,0:T(8,128)S(1)}, f32[8,128]{1,0:T(8,128)S(1)}, u32[]{:S(2)}, u32[]{:S(2)}) collective-permute-start(f32[8,128]{1,0:T(8,128)S(1)} %get-tuple-element.31), channel_id=1, source_target_pairs={{0,2},{1,5},{2,0},{3,7},{4,6},{5,1},{6,4},{7,3},{8,10},{9,13},{10,... | collective-permute-start | bytes 12296 | tf_op jit(solution)/shard_map/ppermute | solution.py:38
  19.0 18.1 %collective-permute-start.7 = (f32[8,16384]{1,0:T(8,128)S(1)}, f32[8,16384]{1,0:T(8,128)S(1)}, u32[]{:S(2)}, u32[]{:S(2)}) collective-permute-start(f32[8,16384]{1,0:T(8,128)S(1)} %get-tuple-element.33), channel_id=1, source_target_pairs={{0,5},{1,4},{2,7},{3,6},{4,1},{5,0},{6,3},{7,2},{8,13},{9,12},{10,... | collective-permute-start | bytes 1572872 | tf_op jit(solution)/shard_map/ppermute | solution.py:38
  19.0 12.4 %collective-permute-start.6 = (f32[8,128]{1,0:T(8,128)S(1)}, f32[8,128]{1,0:T(8,128)S(1)}, u32[]{:S(2)}, u32[]{:S(2)}) collective-permute-start(f32[8,128]{1,0:T(8,128)S(1)} %get-tuple-element.32), channel_id=1, source_target_pairs={{0,4},{1,3},{2,6},{3,1},{4,0},{5,7},{6,2},{7,5},{8,12},{9,11},{10,... | collective-permute-start | bytes 12296 | tf_op jit(solution)/shard_map/ppermute | solution.py:38
  22.1 10.3 %collective-permute-start.8 = (f32[8,128]{1,0:T(8,128)S(1)}, f32[8,128]{1,0:T(8,128)S(1)}, u32[]{:S(2)}, u32[]{:S(2)}) collective-permute-start(f32[8,128]{1,0:T(8,128)S(1)} %get-tuple-element.34), channel_id=1, source_target_pairs={{0,5},{1,4},{2,7},{3,6},{4,1},{5,0},{6,3},{7,2},{8,13},{9,12},{10,... | collective-permute-start | bytes 12296 | tf_op jit(solution)/shard_map/ppermute | solution.py:38
  31.4 36.7 %collective-permute-start.9 = (f32[8,16384]{1,0:T(8,128)S(1)}, f32[8,16384]{1,0:T(8,128)S(1)}, u32[]{:S(2)}, u32[]{:S(2)}) collective-permute-start(f32[8,16384]{1,0:T(8,128)S(1)} %get-tuple-element.35), channel_id=1, source_target_pairs={{0,3},{1,2},{2,1},{3,0},{4,7},{5,6},{6,5},{7,4},{8,11},{9,10},{10,... | collective-permute-start | bytes 1572872 | tf_op jit(solution)/shard_map/ppermute | solution.py:38
  32.4 36.9 %collective-permute-start.11 = (f32[8,16384]{1,0:T(8,128)S(1)}, f32[8,16384]{1,0:T(8,128)S(1)}, u32[]{:S(2)}, u32[]{:S(2)}) collective-permute-start(f32[8,16384]{1,0:T(8,128)S(1)} %get-tuple-element.37), channel_id=1, source_target_pairs={{0,1},{1,0},{2,3},{3,2},{4,5},{5,4},{6,7},{7,6},{8,9},{9,8},{10,11... | collective-permute-start | bytes 1572872 | tf_op jit(solution)/shard_map/ppermute | solution.py:38
  33.0 37.5 %collective-permute-start.12 = (f32[8,16384]{1,0:T(8,128)S(1)}, f32[8,16384]{1,0:T(8,128)S(1)}, u32[]{:S(2)}, u32[]{:S(2)}) collective-permute-start(f32[8,16384]{1,0:T(8,128)S(1)} %get-tuple-element.38), channel_id=1, source_target_pairs={{0,6},{1,7},{2,4},{3,5},{4,2},{5,3},{6,0},{7,1},{8,14},{9,15},{10,... | collective-permute-start | bytes 1572872 | tf_op jit(solution)/shard_map/ppermute | solution.py:38
  35.9 35.8 %collective-permute-start.13 = (f32[8,16384]{1,0:T(8,128)S(1)}, f32[8,16384]{1,0:T(8,128)S(1)}, u32[]{:S(2)}, u32[]{:S(2)}) collective-permute-start(f32[8,16384]{1,0:T(8,128)S(1)} %scan_ahead.1), channel_id=1, source_target_pairs={{0,7},{1,6},{2,5},{3,4},{4,3},{5,2},{6,1},{7,0},{8,15},{9,14},{10,... | collective-permute-start | bytes 1572872 | tf_op jit(solution)/shard_map/ppermute | solution.py:38
  37.1 31.0 %collective-permute-start.10 = (f32[8,128]{1,0:T(8,128)S(1)}, f32[8,128]{1,0:T(8,128)S(1)}, u32[]{:S(2)}, u32[]{:S(2)}) collective-permute-start(f32[8,128]{1,0:T(8,128)S(1)} %get-tuple-element.36), channel_id=1, source_target_pairs={{0,3},{1,2},{2,1},{3,0},{4,7},{5,6},{6,5},{7,4},{8,11},{9,10},{10,... | collective-permute-start | bytes 12296 | tf_op jit(solution)/shard_map/ppermute | solution.py:38
where the time goes:
time: 73.1 us; the launch traced here: 72.5 us
  waiting for transfers between devices  40.5 us (55%)
  starting transfers between devices  19.2 us (26%)
  Pallas kernels  12.7 us (17%)
    ppermute x11, waiting for transfers between devices, swap(): return lax.ppermute(value, 'dev', [(i, i ^ k[i & 1]) for i in range(count)])  39.2 us
    ppermute x11, starting transfers between devices, swap(): return lax.ppermute(value, 'dev', [(i, i ^ k[i & 1]) for i in range(count)])  9.98 us
    ppermute x3, starting transfers between devices, shift_later(): return lax.ppermute(value, 'grp', [(i, i + by) for i in range(count - by)])  9.27 us
    pallas_call x7, Pallas kernels, scan(): pl.pallas_call(functools.partial(scan_kernel, k, len(before), carry is no...  8.17 us
    pallas_call x1, Pallas kernels, sums(): pl.pallas_call(functools.partial(sums_kernel, ahead, rest), out_shape=[sh...  2 us
  transfers between devices with their start and end apart: 14, of which 5 were waited for; matrix products, arithmetic and copies ran while one was open for 0% of the time, Pallas kernels for 15%

commit v1 on v0

--- a/solution.py
+++ b/solution.py
@@ -261,8 +261,8 @@
     )(out, piece)
 
 
-AHEAD, EARLY = [X_OR_Y, Y_OR_X], [Y_OTHER, X_OTHER]
-LATE, LAST = [DIAGONAL, CORE], DIAGONAL_OTHER
+AHEAD, EARLY = [X_OR_Y, Y_OR_X], [Y_OTHER, X_OTHER, DIAGONAL]
+LATE, LAST = [CORE], DIAGONAL_OTHER
 
 
 def overlapped(a):
@@ -281,10 +281,10 @@
         got[k] = swap(value, k)
     got[LAST] = swap(scan_ahead(piece[LAST], carry[LAST]), LAST)
     out = scan(None, SELF, piece[SELF], carry[SELF])
+    for k in LATE:
+        out = scan(out, k, got[k])
     for k in AHEAD + EARLY:
         out = scan(out, k, got[k], got_carry[k])
-    for k in reversed(LATE):
-        out = scan(out, k, got[k])
     return place(out, LAST, got[LAST])
 
 

time: 73.1 us -> 70.1 us (0.959)
  waiting for transfers between devices: 40.5 us -> 29.5 us
  starting transfers between devices: 19.2 us -> 27.6 us
    ppermute x11 -> x12, waiting for transfers between devices: 39.2 us -> 29.5 us  [swap(): return lax.ppermute(value, 'dev', [(i, i ^ k[i & 1]) for i in range(count)])]
    ppermute x11 -> x12, starting transfers between devices: 9.98 us -> 16.8 us  [swap(): return lax.ppermute(value, 'dev', [(i, i ^ k[i & 1]) for i in range(count)])]
    ppermute x3, starting transfers between devices: 9.27 us -> 10.7 us  [shift_later(): return lax.ppermute(value, 'grp', [(i, i + by) for i in range(count - by)])]
    ppermute x3, waiting for transfers between devices: 1.29 us -> 0.01 us  [shift_later(): return lax.ppermute(value, 'grp', [(i, i + by) for i in range(count - by)])]
  transfers between devices with their start and end apart: 14 -> 15, of which waited for: 5 -> 4; matrix products, arithmetic and copies ran while one was open for 0% -> 0% of each run, Pallas kernels for 15% -> 12%
where the time goes in v1:
time: 70.1 us; the launch traced here: 69.9 us
  waiting for transfers between devices  29.5 us (42%)
  starting transfers between devices  27.6 us (39%)
  Pallas kernels  12.7 us (18%)
    ppermute x12, waiting for transfers between devices, swap(): return lax.ppermute(value, 'dev', [(i, i ^ k[i & 1]) for i in range(count)])  29.5 us
    ppermute x12, starting transfers between devices, swap(): return lax.ppermute(value, 'dev', [(i, i ^ k[i & 1]) for i in range(count)])  16.8 us
    ppermute x3, starting transfers between devices, shift_later(): return lax.ppermute(value, 'grp', [(i, i + by) for i in range(count - by)])  10.7 us
    pallas_call x7, Pallas kernels, scan(): pl.pallas_call(functools.partial(scan_kernel, k, len(before), carry is no...  8.15 us
    pallas_call x1, Pallas kernels, sums(): pl.pallas_call(functools.partial(sums_kernel, ahead, rest), out_shape=[sh...  2.01 us
  transfers between devices with their start and end apart: 15, of which 4 were waited for; matrix products, arithmetic and copies ran while one was open for 0% of the time, Pallas kernels for 12%

profile of v1, /device:TPU:0, one launch (start us, length us, event | category | flops | bytes accessed | tf_op | source)
XLA Modules:
  0.0 69.9 jit_solution(487025500070615231)
XLA Ops:
  0.0 1.2 %grab.1 = (f32[8,16384]{1,0:T(8,128)S(1)}, f32[8,16384]{1,0:T(8,128)S(1)}) custom-call(f32[8,131072]{1,0:T(8,128)} %a_ref.3), custom_call_target="tpu_custom_call" | custom-call | flops 1000000 | tf_op jit(solution)/shard_map/grab/pallas_call | solution.py:64
  1.2 2.0 %sums.1 = (f32[8,16384]{1,0:T(8,128)S(1)}, f32[8,16384]{1,0:T(8,128)S(1)}, f32[8,16384]{1,0:T(8,128)S(1)}, f32[8,16384]{1,0:T(8,128)S(1)}, f32[8,16384]{1,0:T(8,...) custom-call(f32[8,131072]{1,0:T(8,128)} %a_ref.3, ...), custom_call_target="tpu_custom_call" | custom-call | flops 40000000 | tf_op jit(solution)/shard_map/sums/pallas_call | solution.py:107
  3.2 7.0 %collective-permute-start.2 = (f32[8,128]{1,0:T(8,128)S(1)}, f32[8,128]{1,0:T(8,128)S(1)}, u32[]{:S(2)}, u32[]{:S(2)}) collective-permute-start(f32[8,128]{1,0:T(8,128)S(1)} %get-tuple-element.27), channel_id=1, source_target_pairs={{0,24},{1,25},{2,26},{3,27},{4,28},{5,29},{6,30},{7,31}} | collective-permute-start | bytes 12296 | tf_op jit(solution)/shard_map/ppermute | solution.py:43
  10.2 1.3 %collective-permute-start.1 = (f32[8,128]{1,0:T(8,128)S(1)}, f32[8,128]{1,0:T(8,128)S(1)}, u32[]{:S(2)}, u32[]{:S(2)}) collective-permute-start(f32[8,128]{1,0:T(8,128)S(1)} %get-tuple-element.27), channel_id=1, source_target_pairs={{0,16},{8,24},{1,17},{9,25},{2,18},{10,26},{3,19},{11,27},{4,20},{... | collective-permute-start | bytes 12296 | tf_op jit(solution)/shard_map/ppermute | solution.py:43
  11.5 2.5 %collective-permute-start = (f32[8,128]{1,0:T(8,128)S(1)}, f32[8,128]{1,0:T(8,128)S(1)}, u32[]{:S(2)}, u32[]{:S(2)}) collective-permute-start(f32[8,128]{1,0:T(8,128)S(1)} %get-tuple-element.27), channel_id=1, source_target_pairs={{0,8},{8,16},{16,24},{1,9},{9,17},{17,25},{2,10},{10,18},{18,26},{... | collective-permute-start | bytes 12296 | tf_op jit(solution)/shard_map/ppermute | solution.py:43
  14.0 1.6 %collective-permute-start.4 = (f32[8,16384]{1,0:T(8,128)S(1)}, f32[8,16384]{1,0:T(8,128)S(1)}, u32[]{:S(2)}, u32[]{:S(2)}) collective-permute-start(f32[8,16384]{1,0:T(8,128)S(1)} %get-tuple-element.23.refs_0_), channel_id=1, source_target_pairs={{0,2},{1,5},{2,0},{3,7},{4,6},{5,1},{6,4},{7,3},{8,10},{9,13},{10,... | collective-permute-start | bytes 1572872 | tf_op jit(solution)/shard_map/ppermute | solution.py:38
  15.6 0.0 collective-permute-done.2.refs_2_
  15.6 0.0 collective-permute-done.1.refs_1_
  15.6 0.0 collective-permute-done.refs_0_
  15.6 0.1 collective-permute-start.3
  15.7 1.3 %collective-permute-start.5 = (f32[8,128]{1,0:T(8,128)S(1)}, f32[8,128]{1,0:T(8,128)S(1)}, u32[]{:S(2)}, u32[]{:S(2)}) collective-permute-start(f32[8,128]{1,0:T(8,128)S(1)} %get-tuple-element.31), channel_id=1, source_target_pairs={{0,2},{1,5},{2,0},{3,7},{4,6},{5,1},{6,4},{7,3},{8,10},{9,13},{10,... | collective-permute-start | bytes 12296 | tf_op jit(solution)/shard_map/ppermute | solution.py:38
  17.0 1.5 %collective-permute-start.7 = (f32[8,128]{1,0:T(8,128)S(1)}, f32[8,128]{1,0:T(8,128)S(1)}, u32[]{:S(2)}, u32[]{:S(2)}) collective-permute-start(f32[8,128]{1,0:T(8,128)S(1)} %get-tuple-element.32), channel_id=1, source_target_pairs={{0,4},{1,3},{2,6},{3,1},{4,0},{5,7},{6,2},{7,5},{8,12},{9,11},{10,... | collective-permute-start | bytes 12296 | tf_op jit(solution)/shard_map/ppermute | solution.py:38
  18.5 0.5 collective-permute-start.6
  19.0 6.7 %collective-permute-done.5.refs_2_ = f32[8,128]{1,0:T(8,128)S(1)} collective-permute-done((f32[8,128]{1,0:T(8,128)S(1)}, f32[8,128]{1,0:T(8,128)S(1)}, u32[]{:S(2)}, u32[]{:S(2)}) %collective-permute-start.5) | collective-permute-done | bytes 4128 | tf_op jit(solution)/shard_map/ppermute | solution.py:38
  25.7 0.0 collective-permute-start.9
  25.7 0.0 collective-permute-done.7.refs_2_
  25.7 1.7 %collective-permute-start.8 = (f32[8,16384]{1,0:T(8,128)S(1)}, f32[8,16384]{1,0:T(8,128)S(1)}, u32[]{:S(2)}, u32[]{:S(2)}) collective-permute-start(f32[8,16384]{1,0:T(8,128)S(1)} %get-tuple-element.33), channel_id=1, source_target_pairs={{0,5},{1,4},{2,7},{3,6},{4,1},{5,0},{6,3},{7,2},{8,13},{9,12},{10,... | collective-permute-start | bytes 1572872 | tf_op jit(solution)/shard_map/ppermute | solution.py:38
  27.5 1.3 %collective-permute-done.9.refs_2_ = f32[8,128]{1,0:T(8,128)S(1)} collective-permute-done((f32[8,128]{1,0:T(8,128)S(1)}, f32[8,128]{1,0:T(8,128)S(1)}, u32[]{:S(2)}, u32[]{:S(2)}) %collective-permute-start.9) | collective-permute-done | bytes 4128 | tf_op jit(solution)/shard_map/ppermute | solution.py:38
  28.8 3.0 %collective-permute-start.10 = (f32[8,16384]{1,0:T(8,128)S(1)}, f32[8,16384]{1,0:T(8,128)S(1)}, u32[]{:S(2)}, u32[]{:S(2)}) collective-permute-start(f32[8,16384]{1,0:T(8,128)S(1)} %get-tuple-element.35), channel_id=1, source_target_pairs={{0,3},{1,2},{2,1},{3,0},{4,7},{5,6},{6,5},{7,4},{8,11},{9,10},{10,... | collective-permute-start | bytes 1572872 | tf_op jit(solution)/shard_map/ppermute | solution.py:38
  31.8 0.0 collective-permute-done.4.refs_1_
  31.8 1.2 %collective-permute-start.12 = (f32[8,16384]{1,0:T(8,128)S(1)}, f32[8,16384]{1,0:T(8,128)S(1)}, u32[]{:S(2)}, u32[]{:S(2)}) collective-permute-start(f32[8,16384]{1,0:T(8,128)S(1)} %get-tuple-element.37), channel_id=1, source_target_pairs={{0,6},{1,7},{2,4},{3,5},{4,2},{5,3},{6,0},{7,1},{8,14},{9,15},{10,... | collective-permute-start | bytes 1572872 | tf_op jit(solution)/shard_map/ppermute | solution.py:38
  33.0 0.5 scan_ahead.1
  33.4 0.0 collective-permute-done.3.refs_1_
  33.4 0.4 collective-permute-start.14
  33.8 1.2 %scan.7.refs_0_ = f32[64,16384]{1,0:T(8,128)} custom-call(f32[8,16384]{1,0:T(8,128)S(1)} %get-tuple-element.25.refs_0_, f32[8,128]{1,0:T(8,128)S(1)} %get-tuple-element.29.refs_1_), custom_call_target="tpu_custom_call" | custom-call | flops 20000000 | tf_op jit(solution)/shard_map/scan/pallas_call | solution.py:213
  35.0 1.2 %scan.8.refs_0_ = f32[64,16384]{1,0:T(8,128)} custom-call(f32[64,16384]{1,0:T(8,128)} %scan.7.refs_0_, f32[8,16384]{1,0:T(8,128)S(1)} %collective-permute-done.3.refs_1_), custom_call_target="tpu_custom_call", output_to_operand_aliasing={{}: (0, {})} | custom-call | flops 20000000 | tf_op jit(solution)/shard_map/scan/pallas_call | solution.py:213
  36.2 0.0 collective-permute-done.6.refs_1_
  36.2 1.2 %collective-permute-start.11 = (f32[8,128]{1,0:T(8,128)S(1)}, f32[8,128]{1,0:T(8,128)S(1)}, u32[]{:S(2)}, u32[]{:S(2)}) collective-permute-start(f32[8,128]{1,0:T(8,128)S(1)} %get-tuple-element.36), channel_id=1, source_target_pairs={{0,3},{1,2},{2,1},{3,0},{4,7},{5,6},{6,5},{7,4},{8,11},{9,10},{10,... | collective-permute-start | bytes 12296 | tf_op jit(solution)/shard_map/ppermute | solution.py:38
  37.4 1.2 %scan.9.refs_0_ = f32[64,16384]{1,0:T(8,128)} custom-call(f32[64,16384]{1,0:T(8,128)} %scan.8.refs_0_, f32[8,16384]{1,0:T(8,128)S(1)} %collective-permute-done.4.refs_1_, f32[8,128]{1,0:T(8,128)S(1)} %collective-permute-done.5.refs_2_), custom_call_target="tpu_custom_call", output_to_operand_aliasing={{}: (0, {})} | custom-call | flops 20000000 | tf_op jit(solution)/shard_map/scan/pallas_call | solution.py:213
  38.6 1.0 %collective-permute-done.8.refs_1_ = f32[8,16384]{1,0:T(8,128)S(1)} collective-permute-done((f32[8,16384]{1,0:T(8,128)S(1)}, f32[8,16384]{1,0:T(8,128)S(1)}, u32[]{:S(2)}, u32[]{:S(2)}) %collective-permute-start.8) | collective-permute-done | bytes 524320 | tf_op jit(solution)/shard_map/ppermute | solution.py:38
  39.6 4.4 %collective-permute-start.13 = (f32[8,128]{1,0:T(8,128)S(1)}, f32[8,128]{1,0:T(8,128)S(1)}, u32[]{:S(2)}, u32[]{:S(2)}) collective-permute-start(f32[8,128]{1,0:T(8,128)S(1)} %get-tuple-element.38), channel_id=1, source_target_pairs={{0,6},{1,7},{2,4},{3,5},{4,2},{5,3},{6,0},{7,1},{8,14},{9,15},{10,... | collective-permute-start | bytes 12296 | tf_op jit(solution)/shard_map/ppermute | solution.py:38
  43.9 1.2 %scan.10.refs_0_ = f32[64,16384]{1,0:T(8,128)} custom-call(f32[64,16384]{1,0:T(8,128)} %scan.9.refs_0_, f32[8,16384]{1,0:T(8,128)S(1)} %collective-permute-done.6.refs_1_, f32[8,128]{1,0:T(8,128)S(1)} %collective-permute-done.7.refs_2_), custom_call_target="tpu_custom_call", output_to_operand_aliasing={{}: (0, {})} | custom-call | flops 20000000 | tf_op jit(solution)/shard_map/scan/pallas_call | solution.py:213
  45.1 1.2 %scan.11.refs_0_ = f32[64,16384]{1,0:T(8,128)} custom-call(f32[64,16384]{1,0:T(8,128)} %scan.10.refs_0_, f32[8,16384]{1,0:T(8,128)S(1)} %collective-permute-done.8.refs_1_, f32[8,128]{1,0:T(8,128)S(1)} %collective-permute-done.9.refs_2_), custom_call_target="tpu_custom_call", output_to_operand_aliasing={{}: (0, {})} | custom-call | flops 20000000 | tf_op jit(solution)/shard_map/scan/pallas_call | solution.py:213
  46.3 20.4 %collective-permute-done.11.refs_2_ = f32[8,128]{1,0:T(8,128)S(1)} collective-permute-done((f32[8,128]{1,0:T(8,128)S(1)}, f32[8,128]{1,0:T(8,128)S(1)}, u32[]{:S(2)}, u32[]{:S(2)}) %collective-permute-start.11) | collective-permute-done | bytes 4128 | tf_op jit(solution)/shard_map/ppermute | solution.py:38
  66.7 0.0 collective-permute-done.10.refs_1_
  66.7 1.2 %scan.12.refs_0_ = f32[64,16384]{1,0:T(8,128)} custom-call(f32[64,16384]{1,0:T(8,128)} %scan.11.refs_0_, f32[8,16384]{1,0:T(8,128)S(1)} %collective-permute-done.10.refs_1_, f32[8,128]{1,0:T(8,128)S(1)} %collective-permute-done.11.refs_2_), custom_call_target="tpu_custom_call", output_to_operand_aliasing={{}: (0, {})} | custom-call | flops 20000000 | tf_op jit(solution)/shard_map/scan/pallas_call | solution.py:213
  67.8 0.0 collective-permute-done.13.refs_2_
  67.9 0.0 collective-permute-done.12.refs_1_
  67.9 1.2 %scan.13._ = f32[64,16384]{1,0:T(8,128)} custom-call(f32[64,16384]{1,0:T(8,128)} %scan.12.refs_0_, f32[8,16384]{1,0:T(8,128)S(1)} %collective-permute-done.12.refs_1_, f32[8,128]{1,0:T(8,128)S(1)} %collective-permute-done.13.refs_2_), custom_call_target="tpu_custom_call", output_to_operand_aliasing={{}: (0, {})} | custom-call | flops 20000000 | tf_op jit(solution)/shard_map/scan/pallas_call | solution.py:213
  69.1 0.0 collective-permute-done.14.piece_ref
  69.1 0.8 %place.1 = f32[64,16384]{1,0:T(8,128)} custom-call(f32[64,16384]{1,0:T(8,128)} %scan.13._, f32[8,16384]{1,0:T(8,128)S(1)} %collective-permute-done.14.piece_ref), custom_call_target="tpu_custom_call", output_to_operand_aliasing={{}: (0, {})} | custom-call | flops 1000000 | tf_op jit(solution)/shard_map/place/pallas_call | solution.py:252
  (1 shorter events, 0.0 us)
Async XLA Ops:
  3.2 12.3 %collective-permute-start.2 = (f32[8,128]{1,0:T(8,128)S(1)}, f32[8,128]{1,0:T(8,128)S(1)}, u32[]{:S(2)}, u32[]{:S(2)}) collective-permute-start(f32[8,128]{1,0:T(8,128)S(1)} %get-tuple-element.27), channel_id=1, source_target_pairs={{0,24},{1,25},{2,26},{3,27},{4,28},{5,29},{6,30},{7,31}} | collective-permute-start | bytes 12296 | tf_op jit(solution)/shard_map/ppermute | solution.py:43
  10.2 5.3 %collective-permute-start.1 = (f32[8,128]{1,0:T(8,128)S(1)}, f32[8,128]{1,0:T(8,128)S(1)}, u32[]{:S(2)}, u32[]{:S(2)}) collective-permute-start(f32[8,128]{1,0:T(8,128)S(1)} %get-tuple-element.27), channel_id=1, source_target_pairs={{0,16},{8,24},{1,17},{9,25},{2,18},{10,26},{3,19},{11,27},{4,20},{... | collective-permute-start | bytes 12296 | tf_op jit(solution)/shard_map/ppermute | solution.py:43
  11.5 4.0 %collective-permute-start = (f32[8,128]{1,0:T(8,128)S(1)}, f32[8,128]{1,0:T(8,128)S(1)}, u32[]{:S(2)}, u32[]{:S(2)}) collective-permute-start(f32[8,128]{1,0:T(8,128)S(1)} %get-tuple-element.27), channel_id=1, source_target_pairs={{0,8},{8,16},{16,24},{1,9},{9,17},{17,25},{2,10},{10,18},{18,26},{... | collective-permute-start | bytes 12296 | tf_op jit(solution)/shard_map/ppermute | solution.py:43
  14.0 17.8 %collective-permute-start.4 = (f32[8,16384]{1,0:T(8,128)S(1)}, f32[8,16384]{1,0:T(8,128)S(1)}, u32[]{:S(2)}, u32[]{:S(2)}) collective-permute-start(f32[8,16384]{1,0:T(8,128)S(1)} %get-tuple-element.23.refs_0_), channel_id=1, source_target_pairs={{0,2},{1,5},{2,0},{3,7},{4,6},{5,1},{6,4},{7,3},{8,10},{9,13},{10,... | collective-permute-start | bytes 1572872 | tf_op jit(solution)/shard_map/ppermute | solution.py:38
  15.6 17.8 %collective-permute-start.3 = (f32[8,16384]{1,0:T(8,128)S(1)}, f32[8,16384]{1,0:T(8,128)S(1)}, u32[]{:S(2)}, u32[]{:S(2)}) collective-permute-start(f32[8,16384]{1,0:T(8,128)S(1)} %get-tuple-element.30), channel_id=1, source_target_pairs={{0,1},{1,0},{2,3},{3,2},{4,5},{5,4},{6,7},{7,6},{8,9},{9,8},{10,11... | collective-permute-start | bytes 1572872 | tf_op jit(solution)/shard_map/ppermute | solution.py:38
  15.7 10.0 %collective-permute-start.5 = (f32[8,128]{1,0:T(8,128)S(1)}, f32[8,128]{1,0:T(8,128)S(1)}, u32[]{:S(2)}, u32[]{:S(2)}) collective-permute-start(f32[8,128]{1,0:T(8,128)S(1)} %get-tuple-element.31), channel_id=1, source_target_pairs={{0,2},{1,5},{2,0},{3,7},{4,6},{5,1},{6,4},{7,3},{8,10},{9,13},{10,... | collective-permute-start | bytes 12296 | tf_op jit(solution)/shard_map/ppermute | solution.py:38
  17.0 8.8 %collective-permute-start.7 = (f32[8,128]{1,0:T(8,128)S(1)}, f32[8,128]{1,0:T(8,128)S(1)}, u32[]{:S(2)}, u32[]{:S(2)}) collective-permute-start(f32[8,128]{1,0:T(8,128)S(1)} %get-tuple-element.32), channel_id=1, source_target_pairs={{0,4},{1,3},{2,6},{3,1},{4,0},{5,7},{6,2},{7,5},{8,12},{9,11},{10,... | collective-permute-start | bytes 12296 | tf_op jit(solution)/shard_map/ppermute | solution.py:38
  18.5 17.7 %collective-permute-start.6 = (f32[8,16384]{1,0:T(8,128)S(1)}, f32[8,16384]{1,0:T(8,128)S(1)}, u32[]{:S(2)}, u32[]{:S(2)}) collective-permute-start(f32[8,16384]{1,0:T(8,128)S(1)} %get-tuple-element.24.refs_1_), channel_id=1, source_target_pairs={{0,4},{1,3},{2,6},{3,1},{4,0},{5,7},{6,2},{7,5},{8,12},{9,11},{10,... | collective-permute-start | bytes 1572872 | tf_op jit(solution)/shard_map/ppermute | solution.py:38
  25.7 3.0 %collective-permute-start.9 = (f32[8,128]{1,0:T(8,128)S(1)}, f32[8,128]{1,0:T(8,128)S(1)}, u32[]{:S(2)}, u32[]{:S(2)}) collective-permute-start(f32[8,128]{1,0:T(8,128)S(1)} %get-tuple-element.34), channel_id=1, source_target_pairs={{0,5},{1,4},{2,7},{3,6},{4,1},{5,0},{6,3},{7,2},{8,13},{9,12},{10,... | collective-permute-start | bytes 12296 | tf_op jit(solution)/shard_map/ppermute | solution.py:38
  25.7 13.8 %collective-permute-start.8 = (f32[8,16384]{1,0:T(8,128)S(1)}, f32[8,16384]{1,0:T(8,128)S(1)}, u32[]{:S(2)}, u32[]{:S(2)}) collective-permute-start(f32[8,16384]{1,0:T(8,128)S(1)} %get-tuple-element.33), channel_id=1, source_target_pairs={{0,5},{1,4},{2,7},{3,6},{4,1},{5,0},{6,3},{7,2},{8,13},{9,12},{10,... | collective-permute-start | bytes 1572872 | tf_op jit(solution)/shard_map/ppermute | solution.py:38
  28.8 37.9 %collective-permute-start.10 = (f32[8,16384]{1,0:T(8,128)S(1)}, f32[8,16384]{1,0:T(8,128)S(1)}, u32[]{:S(2)}, u32[]{:S(2)}) collective-permute-start(f32[8,16384]{1,0:T(8,128)S(1)} %get-tuple-element.35), channel_id=1, source_target_pairs={{0,3},{1,2},{2,1},{3,0},{4,7},{5,6},{6,5},{7,4},{8,11},{9,10},{10,... | collective-permute-start | bytes 1572872 | tf_op jit(solution)/shard_map/ppermute | solution.py:38
  31.8 36.1 %collective-permute-start.12 = (f32[8,16384]{1,0:T(8,128)S(1)}, f32[8,16384]{1,0:T(8,128)S(1)}, u32[]{:S(2)}, u32[]{:S(2)}) collective-permute-start(f32[8,16384]{1,0:T(8,128)S(1)} %get-tuple-element.37), channel_id=1, source_target_pairs={{0,6},{1,7},{2,4},{3,5},{4,2},{5,3},{6,0},{7,1},{8,14},{9,15},{10,... | collective-permute-start | bytes 1572872 | tf_op jit(solution)/shard_map/ppermute | solution.py:38
  33.4 35.6 %collective-permute-start.14 = (f32[8,16384]{1,0:T(8,128)S(1)}, f32[8,16384]{1,0:T(8,128)S(1)}, u32[]{:S(2)}, u32[]{:S(2)}) collective-permute-start(f32[8,16384]{1,0:T(8,128)S(1)} %scan_ahead.1), channel_id=1, source_target_pairs={{0,7},{1,6},{2,5},{3,4},{4,3},{5,2},{6,1},{7,0},{8,15},{9,14},{10,... | collective-permute-start | bytes 1572872 | tf_op jit(solution)/shard_map/ppermute | solution.py:38
  36.2 30.5 %collective-permute-start.11 = (f32[8,128]{1,0:T(8,128)S(1)}, f32[8,128]{1,0:T(8,128)S(1)}, u32[]{:S(2)}, u32[]{:S(2)}) collective-permute-start(f32[8,128]{1,0:T(8,128)S(1)} %get-tuple-element.36), channel_id=1, source_target_pairs={{0,3},{1,2},{2,1},{3,0},{4,7},{5,6},{6,5},{7,4},{8,11},{9,10},{10,... | collective-permute-start | bytes 12296 | tf_op jit(solution)/shard_map/ppermute | solution.py:38
  39.6 28.3 %collective-permute-start.13 = (f32[8,128]{1,0:T(8,128)S(1)}, f32[8,128]{1,0:T(8,128)S(1)}, u32[]{:S(2)}, u32[]{:S(2)}) collective-permute-start(f32[8,128]{1,0:T(8,128)S(1)} %get-tuple-element.38), channel_id=1, source_target_pairs={{0,6},{1,7},{2,4},{3,5},{4,2},{5,3},{6,0},{7,1},{8,14},{9,15},{10,... | collective-permute-start | bytes 12296 | tf_op jit(solution)/shard_map/ppermute | solution.py:38

commit v2 on v1

--- a/solution.py
+++ b/solution.py
@@ -24,7 +24,7 @@
     return jax.ShapeDtypeStruct(dims, jnp.float32)
 
 
-X_OR_Y, Y_OR_X = (2, 4), (4, 2)
+Y, X = (4, 4), (2, 2)
 X_OTHER, Y_OTHER, DIAGONAL, DIAGONAL_OTHER, CORE, SELF = ((k, k) for k in (3, 5, 6, 7, 1, 0))
 
 
@@ -225,32 +225,38 @@
     )(*before, *inputs)
 
 
-def scan_ahead_kernel(piece_ref, carry_ref, out_ref):
-    scan_piece(piece_ref, carry_ref[...], out_ref, lambda at, width: None)
+def scan_ahead_kernel(piece_ref, carry_ref, main_ref, end_ref, held_ref):
+    split = main_ref.shape[1]
+    scan_piece(piece_ref, carry_ref[...], held_ref, lambda at, width: None)
+    main_ref[...] = held_ref[:, :split]
+    end_ref[...] = held_ref[:, split:]
 
 
 def scan_ahead(piece, carry):
+    chans, rows = piece.shape
+    end = rows // 8
     return pl.pallas_call(
         scan_ahead_kernel,
-        out_shape=shape(*piece.shape),
+        out_shape=[shape(chans, rows - end), shape(chans, end)],
         in_specs=[VMEM] * 2,
-        out_specs=VMEM,
+        out_specs=[VMEM] * 2,
+        scratch_shapes=[pltpu.VMEM((chans, rows), jnp.float32)],
         name="scan_ahead",
         **params(8, 20000000),
     )(piece, carry)
 
 
-def place_kernel(k, _, piece_ref, out_ref, sem):
-    chans = piece_ref.shape[0]
+def place_kernel(k, at, _, piece_ref, out_ref, sem):
+    chans, width = piece_ref.shape
     start = pl.multiple_of(partner(k) * chans, chans)
-    copy = pltpu.make_async_copy(piece_ref, out_ref.at[pl.ds(start, chans), :], sem)
+    copy = pltpu.make_async_copy(piece_ref, out_ref.at[pl.ds(start, chans), pl.ds(at, width)], sem)
     copy.start()
     copy.wait()
 
 
-def place(out, k, piece):
-    return pl.pallas_call(
-        functools.partial(place_kernel, k),
+def place(out, k, at, piece):
+    return pl.pallas_call(
+        functools.partial(place_kernel, k, at),
         out_shape=shape(*out.shape),
         in_specs=[HBM, VMEM],
         out_specs=HBM,
@@ -261,7 +267,7 @@
     )(out, piece)
 
 
-AHEAD, EARLY = [X_OR_Y, Y_OR_X], [Y_OTHER, X_OTHER, DIAGONAL]
+AHEAD, EARLY = [Y, X], [Y_OTHER, X_OTHER, DIAGONAL]
 LATE, LAST = [CORE], DIAGONAL_OTHER
 
 
@@ -279,13 +285,15 @@
     got_carry = {k: swap(carry[k], k) for k in AHEAD + EARLY}
     for k, value in zip(LATE, made):
         got[k] = swap(value, k)
-    got[LAST] = swap(scan_ahead(piece[LAST], carry[LAST]), LAST)
+    main, end = scan_ahead(piece[LAST], carry[LAST])
+    main, end = swap(main, LAST), swap(end, LAST)
     out = scan(None, SELF, piece[SELF], carry[SELF])
     for k in LATE:
         out = scan(out, k, got[k])
     for k in AHEAD + EARLY:
         out = scan(out, k, got[k], got_carry[k])
-    return place(out, LAST, got[LAST])
+    out = place(out, LAST, 0, main)
+    return place(out, LAST, main.shape[1], end)
 
 
 def plain(a):

time: 70.1 us -> 66.3 us (0.946)
  starting transfers between devices: 27.6 us -> 21.6 us
  waiting for transfers between devices: 29.5 us -> 31 us
    ppermute x12 -> x13, starting transfers between devices: 16.8 us -> 12.3 us  [swap(): return lax.ppermute(value, 'dev', [(i, i ^ k[i & 1]) for i in range(count)])]
    ppermute x3, starting transfers between devices: 10.7 us -> 9.27 us  [shift_later(): return lax.ppermute(value, 'grp', [(i, i + by) for i in range(count - by)])]
    ppermute x3, waiting for transfers between devices: 0.01 us -> 1.29 us  [shift_later(): return lax.ppermute(value, 'grp', [(i, i + by) for i in range(count - by)])]
    pallas_call x2 -> x3, Pallas kernels: 1.27 us -> 1.9 us  [the longest x2 1.44 us: place(): pl.pallas_call(functools.partial(place_kernel, k, at), out_shape=shape(*o...]
    ppermute x12 -> x13, waiting for transfers between devices: 29.5 us -> 29.7 us  [swap(): return lax.ppermute(value, 'dev', [(i, i ^ k[i & 1]) for i in range(count)])]
  transfers between devices with their start and end apart: 15 -> 16, of which waited for: 4 -> 7; matrix products, arithmetic and copies ran while one was open for 0% -> 0% of each run, Pallas kernels for 12% -> 17%
where the time goes in v2:
time: 66.3 us; the launch traced here: 66.1 us
  waiting for transfers between devices  31 us (47%)
  starting transfers between devices  21.6 us (33%)
  Pallas kernels  13.3 us (20%)
    ppermute x13, waiting for transfers between devices, swap(): return lax.ppermute(value, 'dev', [(i, i ^ k[i & 1]) for i in range(count)])  29.7 us
    ppermute x13, starting transfers between devices, swap(): return lax.ppermute(value, 'dev', [(i, i ^ k[i & 1]) for i in range(count)])  12.3 us
    ppermute x3, starting transfers between devices, shift_later(): return lax.ppermute(value, 'grp', [(i, i + by) for i in range(count - by)])  9.27 us
    pallas_call x7, Pallas kernels, scan(): pl.pallas_call(functools.partial(scan_kernel, k, len(before), carry is no...  8.19 us
    pallas_call x1, Pallas kernels, sums(): pl.pallas_call(functools.partial(sums_kernel, ahead, rest), out_shape=[sh...  2.02 us
    pallas_call x2, Pallas kernels, place(): pl.pallas_call(functools.partial(place_kernel, k, at), out_shape=shape(*o...  1.44 us
  transfers between devices with their start and end apart: 16, of which 7 were waited for; matrix products, arithmetic and copies ran while one was open for 0% of the time, Pallas kernels for 17%

profile of v2, /device:TPU:0, one launch (start us, length us, event | category | flops | bytes accessed | tf_op | source)
XLA Modules:
  0.0 66.1 jit_solution(17716203488680573397)
XLA Ops:
  0.0 1.2 %grab.1 = (f32[8,16384]{1,0:T(8,128)S(1)}, f32[8,16384]{1,0:T(8,128)S(1)}) custom-call(f32[8,131072]{1,0:T(8,128)} %a_ref.3), custom_call_target="tpu_custom_call" | custom-call | flops 1000000 | tf_op jit(solution)/shard_map/grab/pallas_call | solution.py:64
  1.2 3.1 %collective-permute-start.4 = (f32[8,16384]{1,0:T(8,128)S(1)}, f32[8,16384]{1,0:T(8,128)S(1)}, u32[]{:S(2)}, u32[]{:S(2)}) collective-permute-start(f32[8,16384]{1,0:T(8,128)S(1)} %get-tuple-element.25.refs_0_), channel_id=1, source_target_pairs={{0,4},{1,5},{2,6},{3,7},{4,0},{5,1},{6,2},{7,3},{8,12},{9,13},{10,... | collective-permute-start | bytes 1572872 | tf_op jit(solution)/shard_map/ppermute | solution.py:38
  4.3 1.5 %collective-permute-start.6 = (f32[8,16384]{1,0:T(8,128)S(1)}, f32[8,16384]{1,0:T(8,128)S(1)}, u32[]{:S(2)}, u32[]{:S(2)}) collective-permute-start(f32[8,16384]{1,0:T(8,128)S(1)} %get-tuple-element.26.refs_1_), channel_id=1, source_target_pairs={{0,2},{1,3},{2,0},{3,1},{4,6},{5,7},{6,4},{7,5},{8,10},{9,11},{10,... | collective-permute-start | bytes 1572872 | tf_op jit(solution)/shard_map/ppermute | solution.py:38
  5.8 2.0 %sums.1 = (f32[8,16384]{1,0:T(8,128)S(1)}, f32[8,16384]{1,0:T(8,128)S(1)}, f32[8,16384]{1,0:T(8,128)S(1)}, f32[8,16384]{1,0:T(8,128)S(1)}, f32[8,16384]{1,0:T(8,...) custom-call(f32[8,131072]{1,0:T(8,128)} %a_ref.3, ...), custom_call_target="tpu_custom_call" | custom-call | flops 40000000 | tf_op jit(solution)/shard_map/sums/pallas_call | solution.py:107
  7.8 5.5 %collective-permute-start.2 = (f32[8,128]{1,0:T(8,128)S(1)}, f32[8,128]{1,0:T(8,128)S(1)}, u32[]{:S(2)}, u32[]{:S(2)}) collective-permute-start(f32[8,128]{1,0:T(8,128)S(1)} %get-tuple-element.29), channel_id=1, source_target_pairs={{0,24},{1,25},{2,26},{3,27},{4,28},{5,29},{6,30},{7,31}} | collective-permute-start | bytes 12296 | tf_op jit(solution)/shard_map/ppermute | solution.py:43
  13.3 1.3 %collective-permute-start.1 = (f32[8,128]{1,0:T(8,128)S(1)}, f32[8,128]{1,0:T(8,128)S(1)}, u32[]{:S(2)}, u32[]{:S(2)}) collective-permute-start(f32[8,128]{1,0:T(8,128)S(1)} %get-tuple-element.29), channel_id=1, source_target_pairs={{0,16},{8,24},{1,17},{9,25},{2,18},{10,26},{3,19},{11,27},{4,20},{... | collective-permute-start | bytes 12296 | tf_op jit(solution)/shard_map/ppermute | solution.py:43
  14.6 2.5 %collective-permute-start = (f32[8,128]{1,0:T(8,128)S(1)}, f32[8,128]{1,0:T(8,128)S(1)}, u32[]{:S(2)}, u32[]{:S(2)}) collective-permute-start(f32[8,128]{1,0:T(8,128)S(1)} %get-tuple-element.29), channel_id=1, source_target_pairs={{0,8},{8,16},{16,24},{1,9},{9,17},{17,25},{2,10},{10,18},{18,26},{... | collective-permute-start | bytes 12296 | tf_op jit(solution)/shard_map/ppermute | solution.py:43
  17.1 0.0 collective-permute-done.2.refs_2_
  17.1 0.0 collective-permute-done.1.refs_1_
  17.1 1.3 %collective-permute-done.refs_0_ = f32[8,128]{1,0:T(8,128)S(1)} collective-permute-done((f32[8,128]{1,0:T(8,128)S(1)}, f32[8,128]{1,0:T(8,128)S(1)}, u32[]{:S(2)}, u32[]{:S(2)}) %collective-permute-start) | collective-permute-done | bytes 4128 | tf_op jit(solution)/shard_map/ppermute | solution.py:43
  18.4 0.1 collective-permute-start.3
  18.5 0.6 collective-permute-start.5
  19.1 0.5 collective-permute-start.7
  19.6 2.6 %collective-permute-done.5.refs_2_ = f32[8,128]{1,0:T(8,128)S(1)} collective-permute-done((f32[8,128]{1,0:T(8,128)S(1)}, f32[8,128]{1,0:T(8,128)S(1)}, u32[]{:S(2)}, u32[]{:S(2)}) %collective-permute-start.5) | collective-permute-done | bytes 4128 | tf_op jit(solution)/shard_map/ppermute | solution.py:38
  22.2 0.0 collective-permute-start.9
  22.2 0.5 collective-permute-done.7.refs_2_
  22.7 0.3 collective-permute-start.11
  22.9 2.3 %collective-permute-done.9.refs_2_ = f32[8,128]{1,0:T(8,128)S(1)} collective-permute-done((f32[8,128]{1,0:T(8,128)S(1)}, f32[8,128]{1,0:T(8,128)S(1)}, u32[]{:S(2)}, u32[]{:S(2)}) %collective-permute-start.9) | collective-permute-done | bytes 4128 | tf_op jit(solution)/shard_map/ppermute | solution.py:38
  25.2 0.2 collective-permute-start.8
  25.4 0.3 collective-permute-done.11.refs_2_
  25.7 0.3 collective-permute-start.10
  26.0 0.0 collective-permute-done.4.refs_1_
  26.0 2.4 %collective-permute-start.12 = (f32[8,16384]{1,0:T(8,128)S(1)}, f32[8,16384]{1,0:T(8,128)S(1)}, u32[]{:S(2)}, u32[]{:S(2)}) collective-permute-start(f32[8,16384]{1,0:T(8,128)S(1)} %get-tuple-element.39), channel_id=1, source_target_pairs={{0,6},{1,7},{2,4},{3,5},{4,2},{5,3},{6,0},{7,1},{8,14},{9,15},{10,... | collective-permute-start | bytes 1572872 | tf_op jit(solution)/shard_map/ppermute | solution.py:38
  28.4 0.5 scan_ahead.1
  28.9 0.0 collective-permute-done.6.refs_1_
  28.9 0.3 collective-permute-start.14
  29.2 0.0 collective-permute-done.3.refs_1_
  29.2 2.4 %collective-permute-start.15 = (f32[8,2048]{1,0:T(8,128)S(1)}, f32[8,2048]{1,0:T(8,128)S(1)}, u32[]{:S(2)}, u32[]{:S(2)}) collective-permute-start(f32[8,2048]{1,0:T(8,128)S(1)} %get-tuple-element.44), channel_id=1, source_target_pairs={{0,7},{1,6},{2,5},{3,4},{4,3},{5,2},{6,1},{7,0},{8,15},{9,14},{10,... | collective-permute-start | bytes 196616 | tf_op jit(solution)/shard_map/ppermute | solution.py:38
  31.6 1.2 %scan.7.refs_0_ = f32[64,16384]{1,0:T(8,128)} custom-call(f32[8,16384]{1,0:T(8,128)S(1)} %get-tuple-element.27.refs_0_, f32[8,128]{1,0:T(8,128)S(1)} %get-tuple-element.31.refs_1_), custom_call_target="tpu_custom_call" | custom-call | flops 20000000 | tf_op jit(solution)/shard_map/scan/pallas_call | solution.py:213
  32.8 1.2 %scan.8.refs_0_ = f32[64,16384]{1,0:T(8,128)} custom-call(f32[64,16384]{1,0:T(8,128)} %scan.7.refs_0_, f32[8,16384]{1,0:T(8,128)S(1)} %collective-permute-done.3.refs_1_), custom_call_target="tpu_custom_call", output_to_operand_aliasing={{}: (0, {})} | custom-call | flops 20000000 | tf_op jit(solution)/shard_map/scan/pallas_call | solution.py:213
  34.0 1.2 %scan.9.refs_0_ = f32[64,16384]{1,0:T(8,128)} custom-call(f32[64,16384]{1,0:T(8,128)} %scan.8.refs_0_, f32[8,16384]{1,0:T(8,128)S(1)} %collective-permute-done.4.refs_1_, f32[8,128]{1,0:T(8,128)S(1)} %collective-permute-done.5.refs_2_), custom_call_target="tpu_custom_call", output_to_operand_aliasing={{}: (0, {})} | custom-call | flops 20000000 | tf_op jit(solution)/shard_map/scan/pallas_call | solution.py:213
  35.1 3.7 %collective-permute-done.8.refs_1_ = f32[8,16384]{1,0:T(8,128)S(1)} collective-permute-done((f32[8,16384]{1,0:T(8,128)S(1)}, f32[8,16384]{1,0:T(8,128)S(1)}, u32[]{:S(2)}, u32[]{:S(2)}) %collective-permute-start.8) | collective-permute-done | bytes 524320 | tf_op jit(solution)/shard_map/ppermute | solution.py:38
  38.9 0.7 %collective-permute-start.13 = (f32[8,128]{1,0:T(8,128)S(1)}, f32[8,128]{1,0:T(8,128)S(1)}, u32[]{:S(2)}, u32[]{:S(2)}) collective-permute-start(f32[8,128]{1,0:T(8,128)S(1)} %get-tuple-element.40), channel_id=1, source_target_pairs={{0,6},{1,7},{2,4},{3,5},{4,2},{5,3},{6,0},{7,1},{8,14},{9,15},{10,... | collective-permute-start | bytes 12296 | tf_op jit(solution)/shard_map/ppermute | solution.py:38
  39.6 1.2 %scan.10.refs_0_ = f32[64,16384]{1,0:T(8,128)} custom-call(f32[64,16384]{1,0:T(8,128)} %scan.9.refs_0_, f32[8,16384]{1,0:T(8,128)S(1)} %collective-permute-done.6.refs_1_, f32[8,128]{1,0:T(8,128)S(1)} %collective-permute-done.7.refs_2_), custom_call_target="tpu_custom_call", output_to_operand_aliasing={{}: (0, {})} | custom-call | flops 20000000 | tf_op jit(solution)/shard_map/scan/pallas_call | solution.py:213
  40.8 1.2 %scan.11.refs_0_ = f32[64,16384]{1,0:T(8,128)} custom-call(f32[64,16384]{1,0:T(8,128)} %scan.10.refs_0_, f32[8,16384]{1,0:T(8,128)S(1)} %collective-permute-done.8.refs_1_, f32[8,128]{1,0:T(8,128)S(1)} %collective-permute-done.9.refs_2_), custom_call_target="tpu_custom_call", output_to_operand_aliasing={{}: (0, {})} | custom-call | flops 20000000 | tf_op jit(solution)/shard_map/scan/pallas_call | solution.py:213
  42.0 0.0 collective-permute-done.10.refs_1_
  42.0 1.2 %scan.12.refs_0_ = f32[64,16384]{1,0:T(8,128)} custom-call(f32[64,16384]{1,0:T(8,128)} %scan.11.refs_0_, f32[8,16384]{1,0:T(8,128)S(1)} %collective-permute-done.10.refs_1_, f32[8,128]{1,0:T(8,128)S(1)} %collective-permute-done.11.refs_2_), custom_call_target="tpu_custom_call", output_to_operand_aliasing={{}: (0, {})} | custom-call | flops 20000000 | tf_op jit(solution)/shard_map/scan/pallas_call | solution.py:213
  43.2 20.3 %collective-permute-done.13.refs_2_ = f32[8,128]{1,0:T(8,128)S(1)} collective-permute-done((f32[8,128]{1,0:T(8,128)S(1)}, f32[8,128]{1,0:T(8,128)S(1)}, u32[]{:S(2)}, u32[]{:S(2)}) %collective-permute-start.13) | collective-permute-done | bytes 4128 | tf_op jit(solution)/shard_map/ppermute | solution.py:38
  63.5 0.0 collective-permute-done.12.refs_1_
  63.5 1.2 %scan.13._ = f32[64,16384]{1,0:T(8,128)} custom-call(f32[64,16384]{1,0:T(8,128)} %scan.12.refs_0_, f32[8,16384]{1,0:T(8,128)S(1)} %collective-permute-done.12.refs_1_, f32[8,128]{1,0:T(8,128)S(1)} %collective-permute-done.13.refs_2_), custom_call_target="tpu_custom_call", output_to_operand_aliasing={{}: (0, {})} | custom-call | flops 20000000 | tf_op jit(solution)/shard_map/scan/pallas_call | solution.py:213
  64.6 0.0 collective-permute-done.14.piece_ref
  64.6 0.8 %place.2._ = f32[64,16384]{1,0:T(8,128)} custom-call(f32[64,16384]{1,0:T(8,128)} %scan.13._, f32[8,14336]{1,0:T(8,128)S(1)} %collective-permute-done.14.piece_ref), custom_call_target="tpu_custom_call", output_to_operand_aliasing={{}: (0, {})} | custom-call | flops 1000000 | tf_op jit(solution)/shard_map/place/pallas_call | solution.py:258
  65.4 0.0 collective-permute-done.15.piece_ref
  65.5 0.7 place.3
  (1 shorter events, 0.0 us)
Async XLA Ops:
  1.2 24.7 %collective-permute-start.4 = (f32[8,16384]{1,0:T(8,128)S(1)}, f32[8,16384]{1,0:T(8,128)S(1)}, u32[]{:S(2)}, u32[]{:S(2)}) collective-permute-start(f32[8,16384]{1,0:T(8,128)S(1)} %get-tuple-element.25.refs_0_), channel_id=1, source_target_pairs={{0,4},{1,5},{2,6},{3,7},{4,0},{5,1},{6,2},{7,3},{8,12},{9,13},{10,... | collective-permute-start | bytes 1572872 | tf_op jit(solution)/shard_map/ppermute | solution.py:38
  4.3 24.6 %collective-permute-start.6 = (f32[8,16384]{1,0:T(8,128)S(1)}, f32[8,16384]{1,0:T(8,128)S(1)}, u32[]{:S(2)}, u32[]{:S(2)}) collective-permute-start(f32[8,16384]{1,0:T(8,128)S(1)} %get-tuple-element.26.refs_1_), channel_id=1, source_target_pairs={{0,2},{1,3},{2,0},{3,1},{4,6},{5,7},{6,4},{7,5},{8,10},{9,11},{10,... | collective-permute-start | bytes 1572872 | tf_op jit(solution)/shard_map/ppermute | solution.py:38
  7.8 9.3 %collective-permute-start.2 = (f32[8,128]{1,0:T(8,128)S(1)}, f32[8,128]{1,0:T(8,128)S(1)}, u32[]{:S(2)}, u32[]{:S(2)}) collective-permute-start(f32[8,128]{1,0:T(8,128)S(1)} %get-tuple-element.29), channel_id=1, source_target_pairs={{0,24},{1,25},{2,26},{3,27},{4,28},{5,29},{6,30},{7,31}} | collective-permute-start | bytes 12296 | tf_op jit(solution)/shard_map/ppermute | solution.py:43
  13.3 3.8 %collective-permute-start.1 = (f32[8,128]{1,0:T(8,128)S(1)}, f32[8,128]{1,0:T(8,128)S(1)}, u32[]{:S(2)}, u32[]{:S(2)}) collective-permute-start(f32[8,128]{1,0:T(8,128)S(1)} %get-tuple-element.29), channel_id=1, source_target_pairs={{0,16},{8,24},{1,17},{9,25},{2,18},{10,26},{3,19},{11,27},{4,20},{... | collective-permute-start | bytes 12296 | tf_op jit(solution)/shard_map/ppermute | solution.py:43
  14.6 3.8 %collective-permute-start = (f32[8,128]{1,0:T(8,128)S(1)}, f32[8,128]{1,0:T(8,128)S(1)}, u32[]{:S(2)}, u32[]{:S(2)}) collective-permute-start(f32[8,128]{1,0:T(8,128)S(1)} %get-tuple-element.29), channel_id=1, source_target_pairs={{0,8},{8,16},{16,24},{1,9},{9,17},{17,25},{2,10},{10,18},{18,26},{... | collective-permute-start | bytes 12296 | tf_op jit(solution)/shard_map/ppermute | solution.py:43
  18.4 10.7 %collective-permute-start.3 = (f32[8,16384]{1,0:T(8,128)S(1)}, f32[8,16384]{1,0:T(8,128)S(1)}, u32[]{:S(2)}, u32[]{:S(2)}) collective-permute-start(f32[8,16384]{1,0:T(8,128)S(1)} %get-tuple-element.32), channel_id=1, source_target_pairs={{0,1},{1,0},{2,3},{3,2},{4,5},{5,4},{6,7},{7,6},{8,9},{9,8},{10,11... | collective-permute-start | bytes 1572872 | tf_op jit(solution)/shard_map/ppermute | solution.py:38
  18.5 3.7 %collective-permute-start.5 = (f32[8,128]{1,0:T(8,128)S(1)}, f32[8,128]{1,0:T(8,128)S(1)}, u32[]{:S(2)}, u32[]{:S(2)}) collective-permute-start(f32[8,128]{1,0:T(8,128)S(1)} %get-tuple-element.33), channel_id=1, source_target_pairs={{0,4},{1,5},{2,6},{3,7},{4,0},{5,1},{6,2},{7,3},{8,12},{9,13},{10,... | collective-permute-start | bytes 12296 | tf_op jit(solution)/shard_map/ppermute | solution.py:38
  19.1 3.6 %collective-permute-start.7 = (f32[8,128]{1,0:T(8,128)S(1)}, f32[8,128]{1,0:T(8,128)S(1)}, u32[]{:S(2)}, u32[]{:S(2)}) collective-permute-start(f32[8,128]{1,0:T(8,128)S(1)} %get-tuple-element.34), channel_id=1, source_target_pairs={{0,2},{1,3},{2,0},{3,1},{4,6},{5,7},{6,4},{7,5},{8,10},{9,11},{10,... | collective-permute-start | bytes 12296 | tf_op jit(solution)/shard_map/ppermute | solution.py:38
  22.2 3.0 %collective-permute-start.9 = (f32[8,128]{1,0:T(8,128)S(1)}, f32[8,128]{1,0:T(8,128)S(1)}, u32[]{:S(2)}, u32[]{:S(2)}) collective-permute-start(f32[8,128]{1,0:T(8,128)S(1)} %get-tuple-element.36), channel_id=1, source_target_pairs={{0,5},{1,4},{2,7},{3,6},{4,1},{5,0},{6,3},{7,2},{8,13},{9,12},{10,... | collective-permute-start | bytes 12296 | tf_op jit(solution)/shard_map/ppermute | solution.py:38
  22.7 3.0 %collective-permute-start.11 = (f32[8,128]{1,0:T(8,128)S(1)}, f32[8,128]{1,0:T(8,128)S(1)}, u32[]{:S(2)}, u32[]{:S(2)}) collective-permute-start(f32[8,128]{1,0:T(8,128)S(1)} %get-tuple-element.38), channel_id=1, source_target_pairs={{0,3},{1,2},{2,1},{3,0},{4,7},{5,6},{6,5},{7,4},{8,11},{9,10},{10,... | collective-permute-start | bytes 12296 | tf_op jit(solution)/shard_map/ppermute | solution.py:38
  25.2 13.7 %collective-permute-start.8 = (f32[8,16384]{1,0:T(8,128)S(1)}, f32[8,16384]{1,0:T(8,128)S(1)}, u32[]{:S(2)}, u32[]{:S(2)}) collective-permute-start(f32[8,16384]{1,0:T(8,128)S(1)} %get-tuple-element.35), channel_id=1, source_target_pairs={{0,5},{1,4},{2,7},{3,6},{4,1},{5,0},{6,3},{7,2},{8,13},{9,12},{10,... | collective-permute-start | bytes 1572872 | tf_op jit(solution)/shard_map/ppermute | solution.py:38
  25.7 16.2 %collective-permute-start.10 = (f32[8,16384]{1,0:T(8,128)S(1)}, f32[8,16384]{1,0:T(8,128)S(1)}, u32[]{:S(2)}, u32[]{:S(2)}) collective-permute-start(f32[8,16384]{1,0:T(8,128)S(1)} %get-tuple-element.37), channel_id=1, source_target_pairs={{0,3},{1,2},{2,1},{3,0},{4,7},{5,6},{6,5},{7,4},{8,11},{9,10},{10,... | collective-permute-start | bytes 1572872 | tf_op jit(solution)/shard_map/ppermute | solution.py:38
  26.0 37.5 %collective-permute-start.12 = (f32[8,16384]{1,0:T(8,128)S(1)}, f32[8,16384]{1,0:T(8,128)S(1)}, u32[]{:S(2)}, u32[]{:S(2)}) collective-permute-start(f32[8,16384]{1,0:T(8,128)S(1)} %get-tuple-element.39), channel_id=1, source_target_pairs={{0,6},{1,7},{2,4},{3,5},{4,2},{5,3},{6,0},{7,1},{8,14},{9,15},{10,... | collective-permute-start | bytes 1572872 | tf_op jit(solution)/shard_map/ppermute | solution.py:38
  28.9 35.7 %collective-permute-start.14 = (f32[8,14336]{1,0:T(8,128)S(1)}, f32[8,14336]{1,0:T(8,128)S(1)}, u32[]{:S(2)}, u32[]{:S(2)}) collective-permute-start(f32[8,14336]{1,0:T(8,128)S(1)} %get-tuple-element.43), channel_id=1, source_target_pairs={{0,7},{1,6},{2,5},{3,4},{4,3},{5,2},{6,1},{7,0},{8,15},{9,14},{10,... | collective-permute-start | bytes 1376264 | tf_op jit(solution)/shard_map/ppermute | solution.py:38
  29.2 36.3 %collective-permute-start.15 = (f32[8,2048]{1,0:T(8,128)S(1)}, f32[8,2048]{1,0:T(8,128)S(1)}, u32[]{:S(2)}, u32[]{:S(2)}) collective-permute-start(f32[8,2048]{1,0:T(8,128)S(1)} %get-tuple-element.44), channel_id=1, source_target_pairs={{0,7},{1,6},{2,5},{3,4},{4,3},{5,2},{6,1},{7,0},{8,15},{9,14},{10,... | collective-permute-start | bytes 196616 | tf_op jit(solution)/shard_map/ppermute | solution.py:38
  38.9 24.6 %collective-permute-start.13 = (f32[8,128]{1,0:T(8,128)S(1)}, f32[8,128]{1,0:T(8,128)S(1)}, u32[]{:S(2)}, u32[]{:S(2)}) collective-permute-start(f32[8,128]{1,0:T(8,128)S(1)} %get-tuple-element.40), channel_id=1, source_target_pairs={{0,6},{1,7},{2,4},{3,5},{4,2},{5,3},{6,0},{7,1},{8,14},{9,15},{10,... | collective-permute-start | bytes 12296 | tf_op jit(solution)/shard_map/ppermute | solution.py:38
